TPU v7x, 32 devices: a whole 2x2x4 slice. The times are simulated.
32 devices in a mesh: path: 16 (over z, x, core), shard: 2 (over y).
Axes of the slice: x: 2, y: 2, z: 4, core: 2. Of those that a mesh axis runs over, the one named last changes fastest.
Arguments:
- deltas: bfloat16 [16, 32, 4096], P('path', 'shard'), may hold values from -96 to 96
- momentum: float32 [16, 32, 4096], P(None, 'shard', 'path'), may hold values from -4 to 4
- path_module: int32 [16], replicated, may hold values from 0 to 15, as said below
Outputs:
- path_update: bfloat16 [16, 32, 4096], P('path', 'shard')
- new_momentum: float32 [16, 32, 4096], P(None, 'shard', 'path')
Inputs may be any that keep to these rules, and one draw needn't show every extreme that they name: `path_module`: every module is used by at least one and at most seven paths.
All inputs are finite; a program needn't handle non-finite values.
Results may differ from a plain program's by a relative error of at most 0.0004.
Values may be sent and summed in bfloat16 or wider, within the bound.
A program may use at most 64 MiB of HBM per device.

v0:
```python
import jax
import jax.numpy as jnp
from jax import lax
from jax.sharding import PartitionSpec as P

D = 4096
outer_rate = 0.7
momentum_rate = 0.9
clip_ratio = 2.0


def local(deltas, momentum, path_module):
    own_index = lax.axis_index("path")
    modules = momentum.shape[0]
    row_count = deltas.shape[1]
    onehot = (path_module[:, None] == jnp.arange(modules, dtype=jnp.int32)[None, :]).astype(
        jnp.float32
    )
    counts = jnp.sum(onehot, axis=0)
    own_module = lax.dynamic_index_in_dim(path_module, own_index, 0, keepdims=False)
    column_pieces = lax.all_to_all(deltas, "path", split_axis=2, concat_axis=0, tiled=True)
    totals = jnp.einsum(
        "pm,prc->mrc",
        onehot.astype(jnp.bfloat16),
        column_pieces,
        preferred_element_type=jnp.float32,
    )
    outer_grad = totals / counts[:, None, None]
    local_squares = jnp.sum(outer_grad * outer_grad, axis=(1, 2))
    norm_squares = lax.psum(local_squares, ("path", "shard"))
    limit = clip_ratio * jnp.sqrt(jnp.float32(row_count * lax.axis_size("shard") * D))
    shrink = jnp.minimum(1.0, limit / jnp.sqrt(norm_squares + 1e-06))
    clipped = outer_grad * shrink[:, None, None]
    new_momentum = momentum_rate * momentum + clipped
    outer_step = (outer_rate * (clipped + momentum_rate * new_momentum)).astype(jnp.bfloat16)
    gathered = lax.all_gather(outer_step, "path", axis=2, tiled=True)
    path_update = lax.dynamic_index_in_dim(gathered, own_module, 0, keepdims=True)
    return (path_update, new_momentum)


def solution(mesh):
    return jax.shard_map(
        local,
        mesh=mesh,
        in_specs=(P("path", "shard", None), P(None, "shard", "path"), P()),
        out_specs=(P("path", "shard", None), P(None, "shard", "path")),
        check_vma=False,
    )
```

profile of v0, /device:TPU:0, one launch (start us, length us, event | category | flops | bytes accessed | tf_op | source)
XLA Modules:
  0.0 145.2 jit_solution(7055501070345371449)
XLA Ops:
  7.2 4.3 %copy.8 = bf16[1,16,4096]{1,0,2:T(2,128)(2,1)S(1)} copy(bf16[1,16,4096]{2,1,0:T(8,128)(2,1)} %param.3) | data formatting | bytes 262144 | tf_op args[0]
  11.5 0.5 broadcast.26
  12.0 0.0 copy-start.1
  12.0 22.4 %reduce = bf16[4096,16]{1,0:T(8,128)(2,1)S(1)} reduce(bf16[4096,1,16]{2,1,0:T(2,128)(2,1)S(1)} %bitcast.25, bf16[]{:T(256)} %broadcast.26), dimensions={1}, to_apply=%bitcast.15.reduce_sub_computation | reduce | bytes 262146
  34.4 1.8 %reshape.8 = bf16[16,2,2048]{2,1,0:T(2,128)(2,1)} reshape(bf16[4096,16]{1,0:T(8,128)(2,1)S(1)} %reduce) | data formatting | bytes 262144
  36.2 7.4 %all-to-all-start = ((bf16[16,2,2048]{2,1,0:T(2,128)(2,1)}), bf16[16,2,2048]{2,1,0:T(2,128)(2,1)S(1)}, u32[]{:S(2)}, u32[]{:S(2)}) async-start(bf16[16,2,2048]{2,1,0:T(2,128)(2,1)} %reshape.8), calls=%async_computation | async-start | bytes 262144 | tf_op jit(solution)/shard_map/all_to_all | solution.py:21
  43.6 0.0 all-gather.2.cloned.1.call-start
  43.6 0.0 copy-done.1
  43.6 0.1 convert_reduce_fusion
  43.8 7.7 %all-to-all-done = bf16[16,2,2048]{2,1,0:T(2,128)(2,1)S(1)} async-done(((bf16[16,2,2048]{2,1,0:T(2,128)(2,1)}), bf16[16,2,2048]{2,1,0:T(2,128)(2,1)S(1)}, u32[]{:S(2)}, u32[]{:S(2)}) %all-to-all-start) | async-done | bytes 131104 | tf_op jit(solution)/shard_map/all_to_all | solution.py:21
  51.5 1.8 %reshape.9 = bf16[4096,1,16]{2,1,0:T(2,128)(2,1)S(1)} reshape(bf16[16,2,2048]{2,1,0:T(2,128)(2,1)S(1)} %all-to-all-done) | data formatting | bytes 262144
  53.3 0.0 copy-start
  53.3 2.0 %copy.9 = bf16[1,16,4096]{2,1,0:T(8,128)(2,1)S(1)} copy(bf16[1,16,4096]{1,0,2:T(2,128)(2,1)S(1)} %bitcast.26) | data formatting | bytes 262144 | tf_op jit(solution)/shard_map/all_to_all | solution.py:21
  55.3 0.3 multiply_reduce_fusion
  55.6 37.5 %psum.7 = f32[16]{0:T(128)S(1)} all-reduce(f32[16]{0:T(128)S(1)} %get-tuple-element.8), channel_id=1, replica_groups=mesh['path'=16,'shard'=2] {'path','shard'}, use_global_device_ids=true, to_apply=%region_2.3 | all-reduce | flops 16 | bytes 128 | tf_op jit(solution)/shard_map/psum | solution.py:30
  93.1 0.0 copy-done
  93.1 0.9 fusion
  94.0 0.0 all-gather.2.cloned.1.call-update
  94.0 0.6 dynamic_slice.8
  96.5 0.9 copy.12
  97.4 38.6 %all-gather.2.cloned.1.call-done = bf16[16,16,4096]{2,0,1:T(8,128)(2,1)} async-done(((bf16[16,16,256]{2,0,1:T(8,128)(2,1)}), bf16[16,16,4096]{2,0,1:T(8,128)(2,1)}) %all-gather.2.cloned.1.call-update) | async-done | bytes 2097168 | tf_op jit(solution)/shard_map/all_gather | solution.py:36
  136.0 1.5 %constant_dynamic-slice_fusion = bf16[1,16,4096]{2,0,1:T(2,128)(2,1)S(1)} fusion(bf16[16,16,4096]{2,0,1:T(8,128)(2,1)} %all-gather.2.cloned.1.call-done, s32[]{:T(128)S(6)} %select_n.9), kind=kLoop, calls=%fused_computation.12 | loop fusion | bytes 262148 | tf_op jit(solution)/shard_map/jit(dynamic_index_in_dim)/dynamic_slice | solution.py:37
  137.5 0.8 copy.11
  (2 shorter events, 0.0 us)
Async XLA Ops:
  12.0 31.6 %copy-start.1 = (s32[16]{0:T(128)S(1)}, s32[16]{0:T(128)}, u32[]{:S(2)}) copy-start(s32[16]{0:T(128)} %param.5) | copy-start | bytes 196
  36.2 15.3 %all-to-all-start = ((bf16[16,2,2048]{2,1,0:T(2,128)(2,1)}), bf16[16,2,2048]{2,1,0:T(2,128)(2,1)S(1)}, u32[]{:S(2)}, u32[]{:S(2)}) async-start(bf16[16,2,2048]{2,1,0:T(2,128)(2,1)} %reshape.8), calls=%async_computation | async-start | bytes 262144 | tf_op jit(solution)/shard_map/all_to_all | solution.py:21
  43.6 92.4 %all-gather.2.cloned.1.call-start = ((), (), s32[]{:S(2)}) async-start(), calls=%async_computation.1 | async-start | bytes 2228224 | tf_op jit(solution)/shard_map/all_gather | solution.py:36
  53.3 39.8 %copy-start = (f32[16,16,256]{2,1,0:T(8,128)S(1)}, f32[16,16,256]{2,1,0:T(8,128)}, u32[]{:S(2)}) copy-start(f32[16,16,256]{2,1,0:T(8,128)} %param.4) | copy-start | bytes 786436
Sparse Core Ops, SparseCore 0:
  94.1 41.7 all-gather.1
where the time goes:
time: 146 us; the launch traced here: 145 us
  waiting for transfers between devices  46.3 us (32%)
  blocking collectives  37.5 us (26%)
  other arithmetic  23.4 us (16%)
  between operations  16 us (11%)
  local copies, waits for them, and re-layouts  14.2 us (10%)
  starting transfers between devices  7.43 us (5%)
    all_gather x1, waiting for transfers between devices, local(): gathered = lax.all_gather(outer_step, 'path', axis=2, tiled=True)  38.6 us
    psum x1, blocking collectives, local(): norm_squares = lax.psum(local_squares, ('path', 'shard'))  37.5 us
    unnamed x1, other arithmetic  22.4 us
    unnamed x11, local copies, waits for them, and re-layouts  10.1 us
    all_to_all x1, waiting for transfers between devices, local(): lax.all_to_all(deltas, 'path', split_axis=2, concat_axis=0, tiled=True)  7.73 us
    all_to_all x1, starting transfers between devices, local(): lax.all_to_all(deltas, 'path', split_axis=2, concat_axis=0, tiled=True)  7.39 us
  transfers between devices with their start and end apart: 2, of which 2 were waited for; matrix products, arithmetic and copies ran while one was open for 1% of the time, Pallas kernels for 0%

commit v1 on v0

--- a/solution.py
+++ b/solution.py
@@ -33,7 +33,12 @@
     clipped = outer_grad * shrink[:, None, None]
     new_momentum = momentum_rate * momentum + clipped
     outer_step = (outer_rate * (clipped + momentum_rate * new_momentum)).astype(jnp.bfloat16)
-    gathered = lax.all_gather(outer_step, "path", axis=2, tiled=True)
+    ring = [outer_step]
+    for hop in range(15):
+        ring.append(lax.ppermute(ring[-1], "path", [(dev, (dev + 1) % 16) for dev in range(16)]))
+    gathered = jnp.roll(
+        jnp.concatenate(ring[::-1], axis=2), (lax.axis_index("path") + 1) * ring[0].shape[2], axis=2
+    )
     path_update = lax.dynamic_index_in_dim(gathered, own_module, 0, keepdims=True)
     return (path_update, new_momentum)
 

time: 146 us -> 196 us (1.34)
  waiting for transfers between devices: 46.3 us -> 111 us
  between operations: 16 us -> 2.95 us
    ppermute x0 -> x15, waiting for transfers between devices: none -> 103 us  [local(): lax.ppermute(ring[-1], 'path', [(dev, (dev + 1) % 16) for dev in range(16)])]
    all_gather x1 -> x0, waiting for transfers between devices: 38.6 us -> none  [local(): gathered = lax.all_gather(outer_step, 'path', axis=2, tiled=True)]
    unnamed x11 -> x42, local copies, waits for them, and re-layouts: 10.1 us -> 10.4 us
  transfers between devices with their start and end apart: 2 -> 16, of which waited for: 2 -> 16; matrix products, arithmetic and copies ran while one was open for 1% -> 1% of each run, Pallas kernels for 0% -> 0%
where the time goes in v1:
time: 196 us; the launch traced here: 195 us
  waiting for transfers between devices  111 us (57%)
  blocking collectives  37.5 us (19%)
  other arithmetic  22.7 us (12%)
  local copies, waits for them, and re-layouts  13.5 us (7%)
  starting transfers between devices  7.48 us (4%)
  between operations  2.95 us (2%)
    ppermute x15, waiting for transfers between devices, local(): lax.ppermute(ring[-1], 'path', [(dev, (dev + 1) % 16) for dev in range(16)])  103 us
    psum x1, blocking collectives, local(): norm_squares = lax.psum(local_squares, ('path', 'shard'))  37.5 us
    unnamed x1, other arithmetic  22.4 us
    unnamed x42, local copies, waits for them, and re-layouts  10.4 us
    all_to_all x1, waiting for transfers between devices, local(): lax.all_to_all(deltas, 'path', split_axis=2, concat_axis=0, tiled=True)  7.78 us
    all_to_all x1, starting transfers between devices, local(): lax.all_to_all(deltas, 'path', split_axis=2, concat_axis=0, tiled=True)  7.39 us
  transfers between devices with their start and end apart: 16, of which 16 were waited for; matrix products, arithmetic and copies ran while one was open for 1% of the time, Pallas kernels for 0%

profile of v1, /device:TPU:0, one launch (start us, length us, event | category | flops | bytes accessed | tf_op | source)
XLA Modules:
  0.0 195.1 jit_solution(15357455674444460298)
XLA Ops:
  0.6 0.0 copy-start.1
  0.6 4.3 %copy.8 = bf16[1,16,4096]{1,0,2:T(2,128)(2,1)S(1)} copy(bf16[1,16,4096]{2,1,0:T(8,128)(2,1)} %param.3) | data formatting | bytes 262144 | tf_op args[0]
  5.0 0.5 broadcast.27
  5.5 22.4 %reduce = bf16[4096,16]{1,0:T(8,128)(2,1)S(1)} reduce(bf16[4096,1,16]{2,1,0:T(2,128)(2,1)S(1)} %bitcast.25, bf16[]{:T(256)} %broadcast.27), dimensions={1}, to_apply=%bitcast.15.reduce_sub_computation | reduce | bytes 262146
  27.9 0.0 copy-start
  27.9 1.8 reshape.8
  29.7 7.4 %all-to-all-start = ((bf16[16,2,2048]{2,1,0:T(2,128)(2,1)}), bf16[16,2,2048]{2,1,0:T(2,128)(2,1)S(1)}, u32[]{:S(2)}, u32[]{:S(2)}) async-start(bf16[16,2,2048]{2,1,0:T(2,128)(2,1)} %reshape.8), calls=%async_computation | async-start | bytes 262144 | tf_op jit(solution)/shard_map/all_to_all | solution.py:21
  37.1 0.1 convert_reduce_fusion
  37.2 7.8 %all-to-all-done = bf16[16,2,2048]{2,1,0:T(2,128)(2,1)S(1)} async-done(((bf16[16,2,2048]{2,1,0:T(2,128)(2,1)}), bf16[16,2,2048]{2,1,0:T(2,128)(2,1)S(1)}, u32[]{:S(2)}, u32[]{:S(2)}) %all-to-all-start) | async-done | bytes 131104 | tf_op jit(solution)/shard_map/all_to_all | solution.py:21
  45.0 1.8 reshape.9
  46.8 2.0 %copy.9 = bf16[1,16,4096]{2,1,0:T(8,128)(2,1)S(1)} copy(bf16[1,16,4096]{1,0,2:T(2,128)(2,1)S(1)} %bitcast.26) | data formatting | bytes 262144 | tf_op jit(solution)/shard_map/all_to_all | solution.py:21
  48.8 0.3 multiply_reduce_fusion
  49.1 37.5 %psum.7 = f32[16]{0:T(128)S(1)} all-reduce(f32[16]{0:T(128)S(1)} %get-tuple-element.8), channel_id=1, replica_groups=mesh['path'=16,'shard'=2] {'path','shard'}, use_global_device_ids=true, to_apply=%region_2.3 | all-reduce | flops 16 | bytes 128 | tf_op jit(solution)/shard_map/psum | solution.py:30
  86.6 0.2 fusion
  86.8 0.1 collective-permute-start
  86.8 7.1 %collective-permute-done = bf16[16,16,256]{2,0,1:T(8,128)(2,1)S(1)} collective-permute-done((bf16[16,16,256]{2,0,1:T(8,128)(2,1)S(1)}, bf16[16,16,256]{2,0,1:T(8,128)(2,1)S(1)}, u32[]{:S(2)}, u32[]{:S(2)}) %collective-permute-start) | collective-permute-done | bytes 131104 | tf_op jit(solution)/shard_map/ppermute | solution.py:38
  93.9 0.0 collective-permute-start.1
  93.9 7.1 %collective-permute-done.1 = bf16[16,16,256]{2,0,1:T(8,128)(2,1)S(1)} collective-permute-done((bf16[16,16,256]{2,0,1:T(8,128)(2,1)S(1)}, bf16[16,16,256]{2,0,1:T(8,128)(2,1)S(1)}, u32[]{:S(2)}, u32[]{:S(2)}) %collective-permute-start.1) | collective-permute-done | bytes 131104 | tf_op jit(solution)/shard_map/ppermute | solution.py:38
  101.0 0.0 collective-permute-start.2
  101.0 7.1 %collective-permute-done.2 = bf16[16,16,256]{2,0,1:T(8,128)(2,1)S(1)} collective-permute-done((bf16[16,16,256]{2,0,1:T(8,128)(2,1)S(1)}, bf16[16,16,256]{2,0,1:T(8,128)(2,1)S(1)}, u32[]{:S(2)}, u32[]{:S(2)}) %collective-permute-start.2) | collective-permute-done | bytes 131104 | tf_op jit(solution)/shard_map/ppermute | solution.py:38
  108.1 0.0 collective-permute-start.3
  108.1 7.1 %collective-permute-done.3 = bf16[16,16,256]{2,0,1:T(8,128)(2,1)S(1)} collective-permute-done((bf16[16,16,256]{2,0,1:T(8,128)(2,1)S(1)}, bf16[16,16,256]{2,0,1:T(8,128)(2,1)S(1)}, u32[]{:S(2)}, u32[]{:S(2)}) %collective-permute-start.3) | collective-permute-done | bytes 131104 | tf_op jit(solution)/shard_map/ppermute | solution.py:38
  115.2 0.0 collective-permute-start.4
  115.2 7.1 %collective-permute-done.4 = bf16[16,16,256]{2,0,1:T(8,128)(2,1)S(1)} collective-permute-done((bf16[16,16,256]{2,0,1:T(8,128)(2,1)S(1)}, bf16[16,16,256]{2,0,1:T(8,128)(2,1)S(1)}, u32[]{:S(2)}, u32[]{:S(2)}) %collective-permute-start.4) | collective-permute-done | bytes 131104 | tf_op jit(solution)/shard_map/ppermute | solution.py:38
  122.3 0.0 collective-permute-start.5
  122.3 7.1 %collective-permute-done.5 = bf16[16,16,256]{2,0,1:T(8,128)(2,1)S(1)} collective-permute-done((bf16[16,16,256]{2,0,1:T(8,128)(2,1)S(1)}, bf16[16,16,256]{2,0,1:T(8,128)(2,1)S(1)}, u32[]{:S(2)}, u32[]{:S(2)}) %collective-permute-start.5) | collective-permute-done | bytes 131104 | tf_op jit(solution)/shard_map/ppermute | solution.py:38
  129.4 0.0 collective-permute-start.6
  129.4 7.1 %collective-permute-done.6 = bf16[16,16,256]{2,0,1:T(8,128)(2,1)S(1)} collective-permute-done((bf16[16,16,256]{2,0,1:T(8,128)(2,1)S(1)}, bf16[16,16,256]{2,0,1:T(8,128)(2,1)S(1)}, u32[]{:S(2)}, u32[]{:S(2)}) %collective-permute-start.6) | collective-permute-done | bytes 131104 | tf_op jit(solution)/shard_map/ppermute | solution.py:38
  136.5 0.0 collective-permute-start.7
  136.5 7.1 %collective-permute-done.7 = bf16[16,16,256]{2,0,1:T(8,128)(2,1)S(1)} collective-permute-done((bf16[16,16,256]{2,0,1:T(8,128)(2,1)S(1)}, bf16[16,16,256]{2,0,1:T(8,128)(2,1)S(1)}, u32[]{:S(2)}, u32[]{:S(2)}) %collective-permute-start.7) | collective-permute-done | bytes 131104 | tf_op jit(solution)/shard_map/ppermute | solution.py:38
  143.5 0.0 collective-permute-start.8
  143.6 7.1 %collective-permute-done.8 = bf16[16,16,256]{2,0,1:T(8,128)(2,1)S(1)} collective-permute-done((bf16[16,16,256]{2,0,1:T(8,128)(2,1)S(1)}, bf16[16,16,256]{2,0,1:T(8,128)(2,1)S(1)}, u32[]{:S(2)}, u32[]{:S(2)}) %collective-permute-start.8) | collective-permute-done | bytes 131104 | tf_op jit(solution)/shard_map/ppermute | solution.py:38
  150.6 0.0 collective-permute-start.9
  150.6 7.1 %collective-permute-done.9 = bf16[16,16,256]{2,0,1:T(8,128)(2,1)S(1)} collective-permute-done((bf16[16,16,256]{2,0,1:T(8,128)(2,1)S(1)}, bf16[16,16,256]{2,0,1:T(8,128)(2,1)S(1)}, u32[]{:S(2)}, u32[]{:S(2)}) %collective-permute-start.9) | collective-permute-done | bytes 131104 | tf_op jit(solution)/shard_map/ppermute | solution.py:38
  157.7 0.0 collective-permute-start.10
  157.7 7.1 %collective-permute-done.10 = bf16[16,16,256]{2,0,1:T(8,128)(2,1)S(1)} collective-permute-done((bf16[16,16,256]{2,0,1:T(8,128)(2,1)S(1)}, bf16[16,16,256]{2,0,1:T(8,128)(2,1)S(1)}, u32[]{:S(2)}, u32[]{:S(2)}) %collective-permute-start.10) | collective-permute-done | bytes 131104 | tf_op jit(solution)/shard_map/ppermute | solution.py:38
  164.8 0.0 collective-permute-start.11
  164.8 7.1 %collective-permute-done.11 = bf16[16,16,256]{2,0,1:T(8,128)(2,1)S(1)} collective-permute-done((bf16[16,16,256]{2,0,1:T(8,128)(2,1)S(1)}, bf16[16,16,256]{2,0,1:T(8,128)(2,1)S(1)}, u32[]{:S(2)}, u32[]{:S(2)}) %collective-permute-start.11) | collective-permute-done | bytes 131104 | tf_op jit(solution)/shard_map/ppermute | solution.py:38
  171.9 0.0 collective-permute-start.12
  171.9 7.1 %collective-permute-done.12 = bf16[16,16,256]{2,0,1:T(8,128)(2,1)S(1)} collective-permute-done((bf16[16,16,256]{2,0,1:T(8,128)(2,1)S(1)}, bf16[16,16,256]{2,0,1:T(8,128)(2,1)S(1)}, u32[]{:S(2)}, u32[]{:S(2)}) %collective-permute-start.12) | collective-permute-done | bytes 131104 | tf_op jit(solution)/shard_map/ppermute | solution.py:38
  179.0 0.0 collective-permute-start.13
  179.0 7.1 %collective-permute-done.13 = bf16[16,16,256]{2,0,1:T(8,128)(2,1)S(1)} collective-permute-done((bf16[16,16,256]{2,0,1:T(8,128)(2,1)S(1)}, bf16[16,16,256]{2,0,1:T(8,128)(2,1)S(1)}, u32[]{:S(2)}, u32[]{:S(2)}) %collective-permute-start.13) | collective-permute-done | bytes 131104 | tf_op jit(solution)/shard_map/ppermute | solution.py:38
  186.1 0.0 collective-permute-start.14
  186.1 0.6 dynamic_slice.11
  188.6 0.9 copy.12
  189.5 3.7 %collective-permute-done.14 = bf16[16,16,256]{2,0,1:T(8,128)(2,1)S(1)} collective-permute-done((bf16[16,16,256]{2,0,1:T(8,128)(2,1)S(1)}, bf16[16,16,256]{2,0,1:T(8,128)(2,1)S(1)}, u32[]{:S(2)}, u32[]{:S(2)}) %collective-permute-start.14) | collective-permute-done | bytes 131104 | tf_op jit(solution)/shard_map/ppermute | solution.py:38
  193.8 0.5 constant_dynamic-slice_fusion
  194.3 0.8 copy.11
  (36 shorter events, 0.4 us)
Async XLA Ops:
  0.6 36.4 %copy-start.1 = (s32[16]{0:T(128)S(1)}, s32[16]{0:T(128)}, u32[]{:S(2)}) copy-start(s32[16]{0:T(128)} %param.5) | copy-start | bytes 196
  27.9 58.7 %copy-start = (f32[16,16,256]{2,1,0:T(8,128)S(1)}, f32[16,16,256]{2,1,0:T(8,128)}, u32[]{:S(2)}) copy-start(f32[16,16,256]{2,1,0:T(8,128)} %param.4) | copy-start | bytes 786436
  29.7 15.3 %all-to-all-start = ((bf16[16,2,2048]{2,1,0:T(2,128)(2,1)}), bf16[16,2,2048]{2,1,0:T(2,128)(2,1)S(1)}, u32[]{:S(2)}, u32[]{:S(2)}) async-start(bf16[16,2,2048]{2,1,0:T(2,128)(2,1)} %reshape.8), calls=%async_computation | async-start | bytes 262144 | tf_op jit(solution)/shard_map/all_to_all | solution.py:21
  86.8 7.1 %collective-permute-start = (bf16[16,16,256]{2,0,1:T(8,128)(2,1)S(1)}, bf16[16,16,256]{2,0,1:T(8,128)(2,1)S(1)}, u32[]{:S(2)}, u32[]{:S(2)}) collective-permute-start(bf16[16,16,256]{2,0,1:T(8,128)(2,1)S(1)} %get-tuple-element.7), channel_id=1, source_target_pairs={{0,2},{2,4},{4,6},{6,8},{8,10},{10,12},{12,14},{14,16},{16,18},{18... | collective-permute-start | bytes 393224 | tf_op jit(solution)/shard_map/ppermute | solution.py:38
  93.9 7.1 %collective-permute-start.1 = (bf16[16,16,256]{2,0,1:T(8,128)(2,1)S(1)}, bf16[16,16,256]{2,0,1:T(8,128)(2,1)S(1)}, u32[]{:S(2)}, u32[]{:S(2)}) collective-permute-start(bf16[16,16,256]{2,0,1:T(8,128)(2,1)S(1)} %collective-permute-done), channel_id=1, source_target_pairs={{0,2},{2,4},{4,6},{6,8},{8,10},{10,12},{12,14},{14,16},{16,18},{18... | collective-permute-start | bytes 393224 | tf_op jit(solution)/shard_map/ppermute | solution.py:38
  101.0 7.1 %collective-permute-start.2 = (bf16[16,16,256]{2,0,1:T(8,128)(2,1)S(1)}, bf16[16,16,256]{2,0,1:T(8,128)(2,1)S(1)}, u32[]{:S(2)}, u32[]{:S(2)}) collective-permute-start(bf16[16,16,256]{2,0,1:T(8,128)(2,1)S(1)} %collective-permute-done.1), channel_id=1, source_target_pairs={{0,2},{2,4},{4,6},{6,8},{8,10},{10,12},{12,14},{14,16},{16,18},{18... | collective-permute-start | bytes 393224 | tf_op jit(solution)/shard_map/ppermute | solution.py:38
  108.1 7.1 %collective-permute-start.3 = (bf16[16,16,256]{2,0,1:T(8,128)(2,1)S(1)}, bf16[16,16,256]{2,0,1:T(8,128)(2,1)S(1)}, u32[]{:S(2)}, u32[]{:S(2)}) collective-permute-start(bf16[16,16,256]{2,0,1:T(8,128)(2,1)S(1)} %collective-permute-done.2), channel_id=1, source_target_pairs={{0,2},{2,4},{4,6},{6,8},{8,10},{10,12},{12,14},{14,16},{16,18},{18... | collective-permute-start | bytes 393224 | tf_op jit(solution)/shard_map/ppermute | solution.py:38
  115.2 7.1 %collective-permute-start.4 = (bf16[16,16,256]{2,0,1:T(8,128)(2,1)S(1)}, bf16[16,16,256]{2,0,1:T(8,128)(2,1)S(1)}, u32[]{:S(2)}, u32[]{:S(2)}) collective-permute-start(bf16[16,16,256]{2,0,1:T(8,128)(2,1)S(1)} %collective-permute-done.3), channel_id=1, source_target_pairs={{0,2},{2,4},{4,6},{6,8},{8,10},{10,12},{12,14},{14,16},{16,18},{18... | collective-permute-start | bytes 393224 | tf_op jit(solution)/shard_map/ppermute | solution.py:38
  122.3 7.1 %collective-permute-start.5 = (bf16[16,16,256]{2,0,1:T(8,128)(2,1)S(1)}, bf16[16,16,256]{2,0,1:T(8,128)(2,1)S(1)}, u32[]{:S(2)}, u32[]{:S(2)}) collective-permute-start(bf16[16,16,256]{2,0,1:T(8,128)(2,1)S(1)} %collective-permute-done.4), channel_id=1, source_target_pairs={{0,2},{2,4},{4,6},{6,8},{8,10},{10,12},{12,14},{14,16},{16,18},{18... | collective-permute-start | bytes 393224 | tf_op jit(solution)/shard_map/ppermute | solution.py:38
  129.4 7.1 %collective-permute-start.6 = (bf16[16,16,256]{2,0,1:T(8,128)(2,1)S(1)}, bf16[16,16,256]{2,0,1:T(8,128)(2,1)S(1)}, u32[]{:S(2)}, u32[]{:S(2)}) collective-permute-start(bf16[16,16,256]{2,0,1:T(8,128)(2,1)S(1)} %collective-permute-done.5), channel_id=1, source_target_pairs={{0,2},{2,4},{4,6},{6,8},{8,10},{10,12},{12,14},{14,16},{16,18},{18... | collective-permute-start | bytes 393224 | tf_op jit(solution)/shard_map/ppermute | solution.py:38
  136.5 7.1 %collective-permute-start.7 = (bf16[16,16,256]{2,0,1:T(8,128)(2,1)S(1)}, bf16[16,16,256]{2,0,1:T(8,128)(2,1)S(1)}, u32[]{:S(2)}, u32[]{:S(2)}) collective-permute-start(bf16[16,16,256]{2,0,1:T(8,128)(2,1)S(1)} %collective-permute-done.6), channel_id=1, source_target_pairs={{0,2},{2,4},{4,6},{6,8},{8,10},{10,12},{12,14},{14,16},{16,18},{18... | collective-permute-start | bytes 393224 | tf_op jit(solution)/shard_map/ppermute | solution.py:38
  143.5 7.1 %collective-permute-start.8 = (bf16[16,16,256]{2,0,1:T(8,128)(2,1)S(1)}, bf16[16,16,256]{2,0,1:T(8,128)(2,1)S(1)}, u32[]{:S(2)}, u32[]{:S(2)}) collective-permute-start(bf16[16,16,256]{2,0,1:T(8,128)(2,1)S(1)} %collective-permute-done.7), channel_id=1, source_target_pairs={{0,2},{2,4},{4,6},{6,8},{8,10},{10,12},{12,14},{14,16},{16,18},{18... | collective-permute-start | bytes 393224 | tf_op jit(solution)/shard_map/ppermute | solution.py:38
  150.6 7.1 %collective-permute-start.9 = (bf16[16,16,256]{2,0,1:T(8,128)(2,1)S(1)}, bf16[16,16,256]{2,0,1:T(8,128)(2,1)S(1)}, u32[]{:S(2)}, u32[]{:S(2)}) collective-permute-start(bf16[16,16,256]{2,0,1:T(8,128)(2,1)S(1)} %collective-permute-done.8), channel_id=1, source_target_pairs={{0,2},{2,4},{4,6},{6,8},{8,10},{10,12},{12,14},{14,16},{16,18},{18... | collective-permute-start | bytes 393224 | tf_op jit(solution)/shard_map/ppermute | solution.py:38
  157.7 7.1 %collective-permute-start.10 = (bf16[16,16,256]{2,0,1:T(8,128)(2,1)S(1)}, bf16[16,16,256]{2,0,1:T(8,128)(2,1)S(1)}, u32[]{:S(2)}, u32[]{:S(2)}) collective-permute-start(bf16[16,16,256]{2,0,1:T(8,128)(2,1)S(1)} %collective-permute-done.9), channel_id=1, source_target_pairs={{0,2},{2,4},{4,6},{6,8},{8,10},{10,12},{12,14},{14,16},{16,18},{18... | collective-permute-start | bytes 393224 | tf_op jit(solution)/shard_map/ppermute | solution.py:38
  164.8 7.1 %collective-permute-start.11 = (bf16[16,16,256]{2,0,1:T(8,128)(2,1)S(1)}, bf16[16,16,256]{2,0,1:T(8,128)(2,1)S(1)}, u32[]{:S(2)}, u32[]{:S(2)}) collective-permute-start(bf16[16,16,256]{2,0,1:T(8,128)(2,1)S(1)} %collective-permute-done.10), channel_id=1, source_target_pairs={{0,2},{2,4},{4,6},{6,8},{8,10},{10,12},{12,14},{14,16},{16,18},{18... | collective-permute-start | bytes 393224 | tf_op jit(solution)/shard_map/ppermute | solution.py:38
  171.9 7.1 %collective-permute-start.12 = (bf16[16,16,256]{2,0,1:T(8,128)(2,1)S(1)}, bf16[16,16,256]{2,0,1:T(8,128)(2,1)S(1)}, u32[]{:S(2)}, u32[]{:S(2)}) collective-permute-start(bf16[16,16,256]{2,0,1:T(8,128)(2,1)S(1)} %collective-permute-done.11), channel_id=1, source_target_pairs={{0,2},{2,4},{4,6},{6,8},{8,10},{10,12},{12,14},{14,16},{16,18},{18... | collective-permute-start | bytes 393224 | tf_op jit(solution)/shard_map/ppermute | solution.py:38
  179.0 7.1 %collective-permute-start.13 = (bf16[16,16,256]{2,0,1:T(8,128)(2,1)S(1)}, bf16[16,16,256]{2,0,1:T(8,128)(2,1)S(1)}, u32[]{:S(2)}, u32[]{:S(2)}) collective-permute-start(bf16[16,16,256]{2,0,1:T(8,128)(2,1)S(1)} %collective-permute-done.12), channel_id=1, source_target_pairs={{0,2},{2,4},{4,6},{6,8},{8,10},{10,12},{12,14},{14,16},{16,18},{18... | collective-permute-start | bytes 393224 | tf_op jit(solution)/shard_map/ppermute | solution.py:38
  186.1 7.1 %collective-permute-start.14 = (bf16[16,16,256]{2,0,1:T(8,128)(2,1)S(1)}, bf16[16,16,256]{2,0,1:T(8,128)(2,1)S(1)}, u32[]{:S(2)}, u32[]{:S(2)}) collective-permute-start(bf16[16,16,256]{2,0,1:T(8,128)(2,1)S(1)} %collective-permute-done.13), channel_id=1, source_target_pairs={{0,2},{2,4},{4,6},{6,8},{8,10},{10,12},{12,14},{14,16},{16,18},{18... | collective-permute-start | bytes 393224 | tf_op jit(solution)/shard_map/ppermute | solution.py:38
